TPU v7x, 128 devices: a whole 4x4x4 slice. The times are simulated.
128 devices in a mesh: beam: 16 (over z_lo, y, core), hid: 8 (over x, z_hi).
Axes of the slice: x: 4, y: 4, z: 4 (z_hi: 2, z_lo: 2; z = z_hi * 2 + z_lo), core: 2. Of those that a mesh axis runs over, the one named last changes fastest.
Arguments:
- queries: bfloat16 [1024, 256], P('beam'), may hold values from -6 to 6
- beam_ids: int32 [1024, 256], P('beam'), may hold values from 0 to 262143, as said below
- child_table: bfloat16 [524288, 256], P('beam'), may hold values from -6 to 6
- w_query: bfloat16 [256, 1024], P(None, 'hid'), may hold values from -0.21875 to 0.21875
- w_child: bfloat16 [256, 1024], P(None, 'hid'), may hold values from -0.21875 to 0.21875
- w_cross: bfloat16 [256, 1024], P(None, 'hid'), may hold values from -0.21875 to 0.21875
- bias: float32 [1024], P('hid'), may hold values from -3 to 3
- w_out: float32 [1024], P('hid'), may hold values from -0.1875 to 0.1875
Outputs:
- scores: float32 [1024, 512], P('beam', 'hid')
Inputs may be any that keep to these rules, and one draw needn't show every extreme that they name: `beam_ids`: each id b names a node of the current level; its children are rows 2 b and 2 b + 1 of child_table. Among the ids of one index of beam's 64 queries, at most 1536 lie in the rows held by one index of beam (ids r * 16384 to (r + 1) * 16384 - 1 for index r), and in every draw one such index receives exactly 1536 from every index of beam.
All inputs are finite; a program needn't handle non-finite values.
Results may differ from a plain program's by a relative error of at most 0.0019.
Values may be sent and summed in bfloat16 or wider, within the bound.
A program may use at most 128 MiB of HBM per device.

v0:
```python
import math
import jax
import jax.numpy as jnp
from jax import lax
from jax.sharding import PartitionSpec as P


def cut_along(shard, dim, size):
    before, after = (shard.shape[:dim], shard.shape[dim + 1 :])
    return jnp.moveaxis(shard.reshape(*before, size, -1, *after), dim, 0)


def edges_of(length, count):
    hop = length // count
    if hop >= 8:
        hop -= hop % 8
    return [hop * k for k in range(1, count)]


def in_order(pieces, dim):
    pieces = jnp.moveaxis(pieces, 0, dim)
    lengths = pieces.shape
    return pieces.reshape(*lengths[:dim], lengths[dim] * lengths[dim + 1], *lengths[dim + 2 :])


def cut_exchange(shard, axis, pieces, split_dim, concat_dim):
    blocks = cut_along(shard, split_dim, lax.axis_size(axis))
    cut = max(range(1, max(2, blocks.ndim - 1)), key=lambda d: blocks.shape[d])
    gathered = []
    for share in jnp.split(blocks, edges_of(blocks.shape[cut], pieces), axis=cut):
        if share.size:
            gathered.append(lax.all_to_all(share, axis, split_axis=0, concat_axis=0, tiled=True))
    return in_order(jnp.concatenate(gathered, axis=cut), concat_dim)


def sum_at_owner(shard, axis, dim):
    size = lax.axis_size(axis)
    pieces = lax.all_to_all(cut_along(shard, dim, size), axis, 0, 0, tiled=True)
    return jnp.sum(pieces, axis=0)


def owner_ranks(owners, nbeam):
    slots = owners.shape[0]
    block = math.gcd(slots, 512)
    blocks = slots // block
    onehot = (owners[:, None] == jnp.arange(nbeam, dtype=jnp.int32)[None, :]).astype(jnp.bfloat16)
    blocked = onehot.reshape(blocks, block, nbeam)
    lower = (jnp.arange(block)[:, None] > jnp.arange(block)[None, :]).astype(jnp.bfloat16)
    inside = jnp.einsum("ij,bjn->bin", lower, blocked, preferred_element_type=jnp.float32)
    totals = jnp.sum(blocked.astype(jnp.float32), axis=1)
    before = jnp.cumsum(totals, axis=0) - totals
    counts = (inside + before[:, None, :]).reshape(slots, nbeam)
    return jnp.sum(counts * onehot.astype(jnp.float32), axis=1).astype(jnp.int32)


def place_tables(position, offsets, nbeam, capacity):
    slots = position.shape[0]
    index = jnp.arange(slots, dtype=jnp.int32)

    def per_owner(owner):
        wanted = owner * capacity + jnp.arange(capacity, dtype=jnp.int32)
        equal = wanted[:, None] == position[None, :]
        asked = jnp.sum(jnp.where(equal, offsets[None, :], 0), axis=1)
        slot_of = jnp.sum(jnp.where(equal, index[None, :], 0), axis=1)
        live = jnp.any(equal, axis=1).astype(jnp.float32)
        return (asked, slot_of, live)

    return lax.map(per_owner, jnp.arange(nbeam, dtype=jnp.int32))


def shards(queries, beam_ids, child_table, w_query, w_child, w_cross, bias, w_out):
    nbeam = lax.axis_size("beam")
    nhid = lax.axis_size("hid")
    qcount, width = beam_ids.shape
    embed = queries.shape[1]
    slots = qcount * width
    half = child_table.shape[0] // 2
    capacity = 3 * slots // (2 * nbeam)
    pairs_table = child_table.reshape(half, 2 * embed)
    flat_ids = beam_ids.reshape(slots)
    owners = flat_ids // half
    offsets = flat_ids - owners * half
    ranks = owner_ranks(owners, nbeam)
    position = owners * capacity + ranks
    requests, slot_table, live_table = place_tables(position, offsets, nbeam, capacity)
    share = capacity // nhid
    mine = lax.dynamic_slice_in_dim(requests, lax.axis_index("hid") * share, share, 1)
    found = pairs_table[lax.all_to_all(mine, "beam", split_axis=0, concat_axis=0, tiled=True)]
    gotten = cut_exchange(found, "beam", 2, 0, 0)
    fetched = lax.all_gather(gotten, "hid", axis=1, tiled=True)
    received = fetched.reshape(nbeam * capacity, 2 * embed)
    qproj = jnp.dot(queries, w_query, preferred_element_type=jnp.float32) + bias
    block = math.gcd(qcount, max(1, 1024 // width))
    blocks = qcount // block

    def score_block(packed):
        where_rows, qblock, pblock = packed
        rows = received[where_rows].reshape(block, 2 * width, embed)
        cross = (qblock[:, None, :].astype(jnp.float32) * rows.astype(jnp.float32)).astype(
            jnp.bfloat16
        )
        flat_rows = rows.reshape(block * 2 * width, embed)
        flat_cross = cross.reshape(block * 2 * width, embed)
        pre = jnp.dot(flat_rows, w_child, preferred_element_type=jnp.float32) + jnp.dot(
            flat_cross, w_cross, preferred_element_type=jnp.float32
        )
        pre = pre.reshape(block, 2 * width, -1) + pblock[:, None, :]
        return jnp.sum(jnp.maximum(pre, 0.0) * w_out, axis=-1)

    partial_scores = lax.map(
        score_block,
        (
            position.reshape(blocks, block * width),
            queries.reshape(blocks, block, embed),
            qproj.reshape(blocks, block, -1),
        ),
    )
    partial_scores = partial_scores.reshape(qcount, 2 * width)
    return sum_at_owner(partial_scores, "hid", 1)


def solution(mesh):
    return jax.shard_map(
        shards,
        mesh=mesh,
        in_specs=(
            P("beam", None),
            P("beam", None),
            P("beam", None),
            P(None, "hid"),
            P(None, "hid"),
            P(None, "hid"),
            P("hid"),
            P("hid"),
        ),
        out_specs=P("beam", "hid"),
        check_vma=False,
    )
```

profile of v0, /device:TPU:0, one launch (start us, length us, event | category | flops | bytes accessed | tf_op | source)
XLA Modules:
  0.0 969.3 jit_solution(9309029163396406707)
XLA Ops:
  6.5 0.9 reshape.187
  8.4 0.9 copy.24
  9.3 267.1 %while.20 = (s32[]{:T(128)}, s32[16,1536]{1,0:T(8,128)S(1)}, s32[16]{0:T(128)S(1)}, s32[16384]{0:T(1024)S(1)}, s32[16384]{0:T(1024)S(1)}, /*index=5*/s32[]{:T(128)}, s32[1]{0:T(128)}, s32[]{:T(128)}) while((s32[]{:T(128)}, s32[16,1536]{1,0:T(8,128)S(1)}, s32[16]{0:T(128)S(1)}, s32[16384]{0:T(1024)S(1)}, s32[16384]{0:T(1024)S(1)}, ...), condition=%wide.region_5.6_spmd, body=%wide.region_3.5_spmd.sunk | while | flops 75497472 | bytes 174205 | solution.py:68
  10.7 15.1 %select_reduce_fusion.2 = s32[1536]{0:T(1024)S(1)} fusion(s32[16384]{0:T(1024)S(1)} %get-tuple-element.266, s32[16384]{0:T(1024)S(1)} %get-tuple-element.265, s32[1536]{0:T(1024)S(1)} %iota_add_fusion.2), kind=kLoop, calls=%fused_computation.2.clone.1 | loop fusion | flops 75495936 | bytes 143360 | tf_op jit(solution)/shard_map/while/body/eval_jaxpr/reduce_sum | solution.py:63
  27.4 15.1 %select_reduce_fusion.2 = s32[1536]{0:T(1024)S(1)} fusion(s32[16384]{0:T(1024)S(1)} %get-tuple-element.266, s32[16384]{0:T(1024)S(1)} %get-tuple-element.265, s32[1536]{0:T(1024)S(1)} %iota_add_fusion.2), kind=kLoop, calls=%fused_computation.2.clone.1 | loop fusion | flops 75495936 | bytes 143360 | tf_op jit(solution)/shard_map/while/body/eval_jaxpr/reduce_sum | solution.py:63
  44.1 15.1 %select_reduce_fusion.2 = s32[1536]{0:T(1024)S(1)} fusion(s32[16384]{0:T(1024)S(1)} %get-tuple-element.266, s32[16384]{0:T(1024)S(1)} %get-tuple-element.265, s32[1536]{0:T(1024)S(1)} %iota_add_fusion.2), kind=kLoop, calls=%fused_computation.2.clone.1 | loop fusion | flops 75495936 | bytes 143360 | tf_op jit(solution)/shard_map/while/body/eval_jaxpr/reduce_sum | solution.py:63
  60.8 15.1 %select_reduce_fusion.2 = s32[1536]{0:T(1024)S(1)} fusion(s32[16384]{0:T(1024)S(1)} %get-tuple-element.266, s32[16384]{0:T(1024)S(1)} %get-tuple-element.265, s32[1536]{0:T(1024)S(1)} %iota_add_fusion.2), kind=kLoop, calls=%fused_computation.2.clone.1 | loop fusion | flops 75495936 | bytes 143360 | tf_op jit(solution)/shard_map/while/body/eval_jaxpr/reduce_sum | solution.py:63
  77.5 15.1 %select_reduce_fusion.2 = s32[1536]{0:T(1024)S(1)} fusion(s32[16384]{0:T(1024)S(1)} %get-tuple-element.266, s32[16384]{0:T(1024)S(1)} %get-tuple-element.265, s32[1536]{0:T(1024)S(1)} %iota_add_fusion.2), kind=kLoop, calls=%fused_computation.2.clone.1 | loop fusion | flops 75495936 | bytes 143360 | tf_op jit(solution)/shard_map/while/body/eval_jaxpr/reduce_sum | solution.py:63
  94.2 15.1 %select_reduce_fusion.2 = s32[1536]{0:T(1024)S(1)} fusion(s32[16384]{0:T(1024)S(1)} %get-tuple-element.266, s32[16384]{0:T(1024)S(1)} %get-tuple-element.265, s32[1536]{0:T(1024)S(1)} %iota_add_fusion.2), kind=kLoop, calls=%fused_computation.2.clone.1 | loop fusion | flops 75495936 | bytes 143360 | tf_op jit(solution)/shard_map/while/body/eval_jaxpr/reduce_sum | solution.py:63
  110.9 15.1 %select_reduce_fusion.2 = s32[1536]{0:T(1024)S(1)} fusion(s32[16384]{0:T(1024)S(1)} %get-tuple-element.266, s32[16384]{0:T(1024)S(1)} %get-tuple-element.265, s32[1536]{0:T(1024)S(1)} %iota_add_fusion.2), kind=kLoop, calls=%fused_computation.2.clone.1 | loop fusion | flops 75495936 | bytes 143360 | tf_op jit(solution)/shard_map/while/body/eval_jaxpr/reduce_sum | solution.py:63
  127.6 15.1 %select_reduce_fusion.2 = s32[1536]{0:T(1024)S(1)} fusion(s32[16384]{0:T(1024)S(1)} %get-tuple-element.266, s32[16384]{0:T(1024)S(1)} %get-tuple-element.265, s32[1536]{0:T(1024)S(1)} %iota_add_fusion.2), kind=kLoop, calls=%fused_computation.2.clone.1 | loop fusion | flops 75495936 | bytes 143360 | tf_op jit(solution)/shard_map/while/body/eval_jaxpr/reduce_sum | solution.py:63
  144.3 15.1 %select_reduce_fusion.2 = s32[1536]{0:T(1024)S(1)} fusion(s32[16384]{0:T(1024)S(1)} %get-tuple-element.266, s32[16384]{0:T(1024)S(1)} %get-tuple-element.265, s32[1536]{0:T(1024)S(1)} %iota_add_fusion.2), kind=kLoop, calls=%fused_computation.2.clone.1 | loop fusion | flops 75495936 | bytes 143360 | tf_op jit(solution)/shard_map/while/body/eval_jaxpr/reduce_sum | solution.py:63
  161.0 15.1 %select_reduce_fusion.2 = s32[1536]{0:T(1024)S(1)} fusion(s32[16384]{0:T(1024)S(1)} %get-tuple-element.266, s32[16384]{0:T(1024)S(1)} %get-tuple-element.265, s32[1536]{0:T(1024)S(1)} %iota_add_fusion.2), kind=kLoop, calls=%fused_computation.2.clone.1 | loop fusion | flops 75495936 | bytes 143360 | tf_op jit(solution)/shard_map/while/body/eval_jaxpr/reduce_sum | solution.py:63
  177.7 15.1 %select_reduce_fusion.2 = s32[1536]{0:T(1024)S(1)} fusion(s32[16384]{0:T(1024)S(1)} %get-tuple-element.266, s32[16384]{0:T(1024)S(1)} %get-tuple-element.265, s32[1536]{0:T(1024)S(1)} %iota_add_fusion.2), kind=kLoop, calls=%fused_computation.2.clone.1 | loop fusion | flops 75495936 | bytes 143360 | tf_op jit(solution)/shard_map/while/body/eval_jaxpr/reduce_sum | solution.py:63
  194.4 15.1 %select_reduce_fusion.2 = s32[1536]{0:T(1024)S(1)} fusion(s32[16384]{0:T(1024)S(1)} %get-tuple-element.266, s32[16384]{0:T(1024)S(1)} %get-tuple-element.265, s32[1536]{0:T(1024)S(1)} %iota_add_fusion.2), kind=kLoop, calls=%fused_computation.2.clone.1 | loop fusion | flops 75495936 | bytes 143360 | tf_op jit(solution)/shard_map/while/body/eval_jaxpr/reduce_sum | solution.py:63
  211.0 15.1 %select_reduce_fusion.2 = s32[1536]{0:T(1024)S(1)} fusion(s32[16384]{0:T(1024)S(1)} %get-tuple-element.266, s32[16384]{0:T(1024)S(1)} %get-tuple-element.265, s32[1536]{0:T(1024)S(1)} %iota_add_fusion.2), kind=kLoop, calls=%fused_computation.2.clone.1 | loop fusion | flops 75495936 | bytes 143360 | tf_op jit(solution)/shard_map/while/body/eval_jaxpr/reduce_sum | solution.py:63
  227.7 15.1 %select_reduce_fusion.2 = s32[1536]{0:T(1024)S(1)} fusion(s32[16384]{0:T(1024)S(1)} %get-tuple-element.266, s32[16384]{0:T(1024)S(1)} %get-tuple-element.265, s32[1536]{0:T(1024)S(1)} %iota_add_fusion.2), kind=kLoop, calls=%fused_computation.2.clone.1 | loop fusion | flops 75495936 | bytes 143360 | tf_op jit(solution)/shard_map/while/body/eval_jaxpr/reduce_sum | solution.py:63
  244.4 15.1 %select_reduce_fusion.2 = s32[1536]{0:T(1024)S(1)} fusion(s32[16384]{0:T(1024)S(1)} %get-tuple-element.266, s32[16384]{0:T(1024)S(1)} %get-tuple-element.265, s32[1536]{0:T(1024)S(1)} %iota_add_fusion.2), kind=kLoop, calls=%fused_computation.2.clone.1 | loop fusion | flops 75495936 | bytes 143360 | tf_op jit(solution)/shard_map/while/body/eval_jaxpr/reduce_sum | solution.py:63
  261.1 15.1 %select_reduce_fusion.2 = s32[1536]{0:T(1024)S(1)} fusion(s32[16384]{0:T(1024)S(1)} %get-tuple-element.266, s32[16384]{0:T(1024)S(1)} %get-tuple-element.265, s32[1536]{0:T(1024)S(1)} %iota_add_fusion.2), kind=kLoop, calls=%fused_computation.2.clone.1 | loop fusion | flops 75495936 | bytes 143360 | tf_op jit(solution)/shard_map/while/body/eval_jaxpr/reduce_sum | solution.py:63
  277.1 6.0 all-to-all-start
  283.2 24.5 %reshape.188 = bf16[16384,512]{1,0:T(8,128)(2,1)} reshape(bf16[32768,256]{1,0:T(8,128)(2,1)} %param.14) | data formatting | bytes 33554432 | tf_op jit(solution)/shard_map/reshape | solution.py:79
  307.9 19.1 %gather_fusion.1 = bf16[3072,512]{1,0:T(8,128)(2,1)S(1)} fusion(bf16[16384,512]{1,0:T(8,128)(2,1)} %reshape.188, s32[3072]{0:T(1024)S(1)} %broadcast_clamp_fusion.1), kind=kCustom, calls=%fused_computation.1 | custom fusion | bytes 6303744 | tf_op jit(solution)/shard_map/gather | solution.py:88
  327.2 27.6 %all_to_all.27 = bf16[16,1,96,512]{3,2,1,0:T(8,128)(2,1)S(1)} all-to-all(bf16[16,1,96,512]{3,2,1,0:T(8,128)(2,1)S(1)} %get-tuple-element.155), channel_id=1, replica_groups=mesh['beam'=16,'hid'=8] {'beam'}, dimensions={0} | all-to-all | bytes 3145728 | tf_op jit(solution)/shard_map/all_to_all | solution.py:32
  354.8 24.7 %all_to_all.28 = bf16[16,1,96,512]{3,2,1,0:T(8,128)(2,1)S(1)} all-to-all(bf16[16,1,96,512]{3,2,1,0:T(8,128)(2,1)S(1)} %get-tuple-element.154), channel_id=1, replica_groups=mesh['beam'=16,'hid'=8] {'beam'}, dimensions={0} | all-to-all | bytes 3145728 | tf_op jit(solution)/shard_map/all_to_all | solution.py:32
  379.5 2.0 pad_maximum_fusion
  381.5 0.8 copy-done.4
  383.0 0.7 convolution_add_fusion.2
  383.8 259.6 %all-gather.3.cloned.1.call-done = bf16[16,1,1536,512]{3,2,1,0:T(8,128)(2,1)} async-done(((bf16[16,1,192,512]{3,2,1,0:T(8,128)(2,1)}), bf16[16,1,1536,512]{3,2,1,0:T(8,128)(2,1)}) %all-gather.3.cloned.1.call-update) | async-done | bytes 25165840 | tf_op jit(solution)/shard_map/all_gather | solution.py:90
  643.4 306.0 %while.21 = (s32[]{:T(128)}, f32[16,4,512]{2,1,0:T(4,128)S(1)}, s32[16,1024]{1,0:T(8,128)S(1)}, bf16[24576,512]{1,0:T(8,128)(2,1)}, bf16[256,128]{1,0:T(8,128)(2...) while((s32[]{:T(128)}, f32[16,4,512]{2,1,0:T(4,128)S(1)}, ...), condition=%wide.region_8.9_spmd, body=%wide.region_6.8_spmd.sunk | while | flops 271322112 | bytes 14893693 | solution.py:110
  644.8 15.4 %gather_fusion = bf16[1024,512]{1,0:T(8,128)(2,1)S(1)} fusion(bf16[24576,512]{1,0:T(8,128)(2,1)} %get-tuple-element.293, s32[1024]{0:T(1024)S(1)} %broadcast_clamp_fusion.3), kind=kCustom, calls=%fused_computation.clone.1 | custom fusion | bytes 2101248 | tf_op jit(solution)/shard_map/while/body/eval_jaxpr/gather | solution.py:98
  663.9 15.4 %gather_fusion = bf16[1024,512]{1,0:T(8,128)(2,1)S(1)} fusion(bf16[24576,512]{1,0:T(8,128)(2,1)} %get-tuple-element.293, s32[1024]{0:T(1024)S(1)} %broadcast_clamp_fusion.3), kind=kCustom, calls=%fused_computation.clone.1 | custom fusion | bytes 2101248 | tf_op jit(solution)/shard_map/while/body/eval_jaxpr/gather | solution.py:98
  683.1 15.4 %gather_fusion = bf16[1024,512]{1,0:T(8,128)(2,1)S(1)} fusion(bf16[24576,512]{1,0:T(8,128)(2,1)} %get-tuple-element.293, s32[1024]{0:T(1024)S(1)} %broadcast_clamp_fusion.3), kind=kCustom, calls=%fused_computation.clone.1 | custom fusion | bytes 2101248 | tf_op jit(solution)/shard_map/while/body/eval_jaxpr/gather | solution.py:98
  699.4 0.7 bitcast_convert_fusion.2
  702.2 15.4 %gather_fusion = bf16[1024,512]{1,0:T(8,128)(2,1)S(1)} fusion(bf16[24576,512]{1,0:T(8,128)(2,1)} %get-tuple-element.293, s32[1024]{0:T(1024)S(1)} %broadcast_clamp_fusion.3), kind=kCustom, calls=%fused_computation.clone.1 | custom fusion | bytes 2101248 | tf_op jit(solution)/shard_map/while/body/eval_jaxpr/gather | solution.py:98
  721.3 15.4 %gather_fusion = bf16[1024,512]{1,0:T(8,128)(2,1)S(1)} fusion(bf16[24576,512]{1,0:T(8,128)(2,1)} %get-tuple-element.293, s32[1024]{0:T(1024)S(1)} %broadcast_clamp_fusion.3), kind=kCustom, calls=%fused_computation.clone.1 | custom fusion | bytes 2101248 | tf_op jit(solution)/shard_map/while/body/eval_jaxpr/gather | solution.py:98
  740.5 15.4 %gather_fusion = bf16[1024,512]{1,0:T(8,128)(2,1)S(1)} fusion(bf16[24576,512]{1,0:T(8,128)(2,1)} %get-tuple-element.293, s32[1024]{0:T(1024)S(1)} %broadcast_clamp_fusion.3), kind=kCustom, calls=%fused_computation.clone.1 | custom fusion | bytes 2101248 | tf_op jit(solution)/shard_map/while/body/eval_jaxpr/gather | solution.py:98
  759.5 15.4 %gather_fusion = bf16[1024,512]{1,0:T(8,128)(2,1)S(1)} fusion(bf16[24576,512]{1,0:T(8,128)(2,1)} %get-tuple-element.293, s32[1024]{0:T(1024)S(1)} %broadcast_clamp_fusion.3), kind=kCustom, calls=%fused_computation.clone.1 | custom fusion | bytes 2101248 | tf_op jit(solution)/shard_map/while/body/eval_jaxpr/gather | solution.py:98
  778.7 15.4 %gather_fusion = bf16[1024,512]{1,0:T(8,128)(2,1)S(1)} fusion(bf16[24576,512]{1,0:T(8,128)(2,1)} %get-tuple-element.293, s32[1024]{0:T(1024)S(1)} %broadcast_clamp_fusion.3), kind=kCustom, calls=%fused_computation.clone.1 | custom fusion | bytes 2101248 | tf_op jit(solution)/shard_map/while/body/eval_jaxpr/gather | solution.py:98
  797.8 15.4 %gather_fusion = bf16[1024,512]{1,0:T(8,128)(2,1)S(1)} fusion(bf16[24576,512]{1,0:T(8,128)(2,1)} %get-tuple-element.293, s32[1024]{0:T(1024)S(1)} %broadcast_clamp_fusion.3), kind=kCustom, calls=%fused_computation.clone.1 | custom fusion | bytes 2101248 | tf_op jit(solution)/shard_map/while/body/eval_jaxpr/gather | solution.py:98
  816.9 15.4 %gather_fusion = bf16[1024,512]{1,0:T(8,128)(2,1)S(1)} fusion(bf16[24576,512]{1,0:T(8,128)(2,1)} %get-tuple-element.293, s32[1024]{0:T(1024)S(1)} %broadcast_clamp_fusion.3), kind=kCustom, calls=%fused_computation.clone.1 | custom fusion | bytes 2101248 | tf_op jit(solution)/shard_map/while/body/eval_jaxpr/gather | solution.py:98
  836.0 15.4 %gather_fusion = bf16[1024,512]{1,0:T(8,128)(2,1)S(1)} fusion(bf16[24576,512]{1,0:T(8,128)(2,1)} %get-tuple-element.293, s32[1024]{0:T(1024)S(1)} %broadcast_clamp_fusion.3), kind=kCustom, calls=%fused_computation.clone.1 | custom fusion | bytes 2101248 | tf_op jit(solution)/shard_map/while/body/eval_jaxpr/gather | solution.py:98
  855.1 15.4 %gather_fusion = bf16[1024,512]{1,0:T(8,128)(2,1)S(1)} fusion(bf16[24576,512]{1,0:T(8,128)(2,1)} %get-tuple-element.293, s32[1024]{0:T(1024)S(1)} %broadcast_clamp_fusion.3), kind=kCustom, calls=%fused_computation.clone.1 | custom fusion | bytes 2101248 | tf_op jit(solution)/shard_map/while/body/eval_jaxpr/gather | solution.py:98
  874.2 15.4 %gather_fusion = bf16[1024,512]{1,0:T(8,128)(2,1)S(1)} fusion(bf16[24576,512]{1,0:T(8,128)(2,1)} %get-tuple-element.293, s32[1024]{0:T(1024)S(1)} %broadcast_clamp_fusion.3), kind=kCustom, calls=%fused_computation.clone.1 | custom fusion | bytes 2101248 | tf_op jit(solution)/shard_map/while/body/eval_jaxpr/gather | solution.py:98
  893.4 15.4 %gather_fusion = bf16[1024,512]{1,0:T(8,128)(2,1)S(1)} fusion(bf16[24576,512]{1,0:T(8,128)(2,1)} %get-tuple-element.293, s32[1024]{0:T(1024)S(1)} %broadcast_clamp_fusion.3), kind=kCustom, calls=%fused_computation.clone.1 | custom fusion | bytes 2101248 | tf_op jit(solution)/shard_map/while/body/eval_jaxpr/gather | solution.py:98
  912.5 15.4 %gather_fusion = bf16[1024,512]{1,0:T(8,128)(2,1)S(1)} fusion(bf16[24576,512]{1,0:T(8,128)(2,1)} %get-tuple-element.293, s32[1024]{0:T(1024)S(1)} %broadcast_clamp_fusion.3), kind=kCustom, calls=%fused_computation.clone.1 | custom fusion | bytes 2101248 | tf_op jit(solution)/shard_map/while/body/eval_jaxpr/gather | solution.py:98
  931.7 15.4 %gather_fusion = bf16[1024,512]{1,0:T(8,128)(2,1)S(1)} fusion(bf16[24576,512]{1,0:T(8,128)(2,1)} %get-tuple-element.293, s32[1024]{0:T(1024)S(1)} %broadcast_clamp_fusion.3), kind=kCustom, calls=%fused_computation.clone.1 | custom fusion | bytes 2101248 | tf_op jit(solution)/shard_map/while/body/eval_jaxpr/gather | solution.py:98
  949.8 10.5 %all_to_all.29 = f32[8,1,4096]{2,1,0:T(1,128)S(1)} all-to-all(f32[8,1,4096]{2,1,0:T(1,128)S(1)} %reshape.218), channel_id=1, replica_groups=mesh['beam'=16,'hid'=8] {'hid'}, dimensions={0} | all-to-all | bytes 262144 | tf_op jit(solution)/shard_map/all_to_all | solution.py:38
  960.8 1.0 reduce.4
  (316 shorter events, 75.7 us)
Async XLA Ops:
  6.5 376.4 %copy-start = (bf16[256,128]{1,0:T(8,128)(2,1)S(1)}, bf16[256,128]{1,0:T(8,128)(2,1)}, u32[]{:S(2)}) copy-start(bf16[256,128]{1,0:T(8,128)(2,1)} %param.15) | copy-start | bytes 196612
  277.1 30.6 %all-to-all-start = ((s32[16,1,192]{2,1,0:T(1,128)}), s32[16,1,192]{2,1,0:T(1,128)S(1)}, u32[]{:S(2)}, u32[]{:S(2)}) async-start(s32[16,1,192]{2,1,0:T(1,128)} %all_to_all.17), calls=%async_computation | async-start | bytes 32768 | tf_op jit(solution)/shard_map/all_to_all | solution.py:88
  283.2 360.2 %all-gather.3.cloned.1.call-start = ((), (), s32[]{:S(2)}) async-start(), calls=%async_computation.4 | async-start | bytes 28311552 | tf_op jit(solution)/shard_map/all_gather | solution.py:90
  381.4 0.8 copy-start.4
  381.4 0.9 copy-start.5
  381.4 1.5 copy-start.7
  381.5 262.0 %copy-start.2 = (bf16[256,128]{1,0:T(8,128)(2,1)S(1)}, bf16[256,128]{1,0:T(8,128)(2,1)}, u32[]{:S(2)}) copy-start(bf16[256,128]{1,0:T(8,128)(2,1)} %param.16) | copy-start | bytes 196612
  381.5 262.0 %copy-start.3 = (bf16[256,128]{1,0:T(8,128)(2,1)S(1)}, bf16[256,128]{1,0:T(8,128)(2,1)}, u32[]{:S(2)}) copy-start(bf16[256,128]{1,0:T(8,128)(2,1)} %param.17) | copy-start | bytes 196612
  381.5 262.0 %copy-start.6 = (f32[128]{0:T(128)S(1)}, f32[128]{0:T(128)}, u32[]{:S(2)}) copy-start(f32[128]{0:T(128)} %param.19) | copy-start | bytes 1540
  949.4 13.1 %copy-start.1 = (bf16[256,128]{1,0:T(8,128)(2,1)S(1)}, bf16[256,128]{1,0:T(8,128)(2,1)}, u32[]{:S(2)}) copy-start(bf16[256,128]{1,0:T(8,128)(2,1)} %param.15) | copy-start | bytes 196612
Sparse Core Ops, SparseCore 0:
  381.6 261.7 all-gather.2
where the time goes:
time: 972 us; the launch traced here: 969 us
  local copies, waits for them, and re-layouts  336 us (35%)
  other arithmetic  261 us (27%)
  waiting for transfers between devices  260 us (27%)
  blocking collectives  62.7 us (6%)
  matrix products  17.4 us (2%)
  between operations  13.6 us (1%)
  loops' own time  13.2 us (1%)
    all_gather x1, waiting for transfers between devices, shards(): fetched = lax.all_gather(gotten, 'hid', axis=1, tiled=True)  260 us
    gather x16, local copies, waits for them, and re-layouts, score_block(): rows = received[where_rows].reshape(block, 2 * width, embed)  246 us
    reduce_sum x16, other arithmetic, per_owner(): asked = jnp.sum(jnp.where(equal, offsets[None, :], 0), axis=1)  242 us
    all_to_all x2, blocking collectives, cut_exchange(): lax.all_to_all(share, axis, split_axis=0, concat_axis=0, tiled=True)  52.3 us
    reshape x1, local copies, waits for them, and re-layouts, shards(): pairs_table = child_table.reshape(half, 2 * embed)  24.5 us
  transfers between devices with their start and end apart: 2, of which 1 were waited for; matrix products, arithmetic and copies ran while one was open for 3% of the time, Pallas kernels for 0%

commit v1 on v0

--- a/solution.py
+++ b/solution.py
@@ -87,7 +87,9 @@
     mine = lax.dynamic_slice_in_dim(requests, lax.axis_index("hid") * share, share, 1)
     found = pairs_table[lax.all_to_all(mine, "beam", split_axis=0, concat_axis=0, tiled=True)]
     gotten = cut_exchange(found, "beam", 2, 0, 0)
-    fetched = lax.all_gather(gotten, "hid", axis=1, tiled=True)
+    fetched = jnp.concatenate(
+        lax.all_to_all(jnp.stack([gotten] * lax.axis_size("hid")), "hid", 0, 0), axis=1
+    )
     received = fetched.reshape(nbeam * capacity, 2 * embed)
     qproj = jnp.dot(queries, w_query, preferred_element_type=jnp.float32) + bias
     block = math.gcd(qcount, max(1, 1024 // width))

time: 972 us -> 1070 us (1.10)
  waiting for transfers between devices: 260 us -> 338 us
  local copies, waits for them, and re-layouts: 336 us -> 365 us
  between operations: 13.6 us -> 0.22 us
    all_to_all x0 -> x1, waiting for transfers between devices: none -> 338 us  [shards(): lax.all_to_all(jnp.stack([gotten] * lax.axis_size('hid')), 'hid', 0, 0)]
    all_gather x1 -> x0, waiting for transfers between devices: 260 us -> none  [shards(): fetched = lax.all_gather(gotten, 'hid', axis=1, tiled=True)]
    all_to_all x0 -> x1, local copies, waits for them, and re-layouts: none -> 21 us  [shards(): lax.all_to_all(jnp.stack([gotten] * lax.axis_size('hid')), 'hid', 0, 0)]
  transfers between devices with their start and end apart: 2 -> 2, of which waited for: 1 -> 1; matrix products, arithmetic and copies ran while one was open for 3% -> 2% of each run, Pallas kernels for 0% -> 0%
where the time goes in v1:
time: 1070 us
  local copies, waits for them, and re-layouts  365 us (34%)
  waiting for transfers between devices  338 us (32%)
  other arithmetic  259 us (24%)
  blocking collectives  64.7 us (6%)
  matrix products  17.3 us (2%)
  starting transfers between devices  13.5 us (1%)
  loops' own time  13.2 us (1%)
    all_to_all x1, waiting for transfers between devices, shards(): lax.all_to_all(jnp.stack([gotten] * lax.axis_size('hid')), 'hid', 0, 0)  338 us
    gather x16, local copies, waits for them, and re-layouts, score_block(): rows = received[where_rows].reshape(block, 2 * width, embed)  246 us
    reduce_sum x16, other arithmetic, per_owner(): asked = jnp.sum(jnp.where(equal, offsets[None, :], 0), axis=1)  242 us
    all_to_all x2, blocking collectives, cut_exchange(): lax.all_to_all(share, axis, split_axis=0, concat_axis=0, tiled=True)  52.3 us
    reshape x1, local copies, waits for them, and re-layouts, shards(): pairs_table = child_table.reshape(half, 2 * embed)  24.5 us
  transfers between devices with their start and end apart: 2, of which 1 were waited for; matrix products, arithmetic and copies ran while one was open for 2% of the time, Pallas kernels for 0%

profile of v1, /device:TPU:0, one launch (start us, length us, event | category | flops | bytes accessed | tf_op | source)
XLA Modules:
  0.0 1070.7 jit_solution(6186964880532380224)
XLA Ops:
  0.0 0.9 reshape.186
  1.9 0.9 copy.26
  2.8 267.1 %while.20 = (s32[]{:T(128)}, s32[16,1536]{1,0:T(8,128)S(1)}, s32[16]{0:T(128)S(1)}, s32[16384]{0:T(1024)S(1)}, s32[16384]{0:T(1024)S(1)}, /*index=5*/s32[]{:T(128)}, s32[1]{0:T(128)}, s32[]{:T(128)}) while((s32[]{:T(128)}, s32[16,1536]{1,0:T(8,128)S(1)}, s32[16]{0:T(128)S(1)}, s32[16384]{0:T(1024)S(1)}, s32[16384]{0:T(1024)S(1)}, ...), condition=%wide.region_5.6_spmd, body=%wide.region_3.5_spmd.sunk | while | flops 75497472 | bytes 174197 | solution.py:68
  4.2 15.1 %select_reduce_fusion.2 = s32[1536]{0:T(1024)S(1)} fusion(s32[16384]{0:T(1024)S(1)} %get-tuple-element.266, s32[16384]{0:T(1024)S(1)} %get-tuple-element.265, s32[1536]{0:T(1024)S(1)} %iota_add_fusion.2), kind=kLoop, calls=%fused_computation.2.clone.1 | loop fusion | flops 75495936 | bytes 143360 | tf_op jit(solution)/shard_map/while/body/eval_jaxpr/reduce_sum | solution.py:63
  20.9 15.1 %select_reduce_fusion.2 = s32[1536]{0:T(1024)S(1)} fusion(s32[16384]{0:T(1024)S(1)} %get-tuple-element.266, s32[16384]{0:T(1024)S(1)} %get-tuple-element.265, s32[1536]{0:T(1024)S(1)} %iota_add_fusion.2), kind=kLoop, calls=%fused_computation.2.clone.1 | loop fusion | flops 75495936 | bytes 143360 | tf_op jit(solution)/shard_map/while/body/eval_jaxpr/reduce_sum | solution.py:63
  37.6 15.1 %select_reduce_fusion.2 = s32[1536]{0:T(1024)S(1)} fusion(s32[16384]{0:T(1024)S(1)} %get-tuple-element.266, s32[16384]{0:T(1024)S(1)} %get-tuple-element.265, s32[1536]{0:T(1024)S(1)} %iota_add_fusion.2), kind=kLoop, calls=%fused_computation.2.clone.1 | loop fusion | flops 75495936 | bytes 143360 | tf_op jit(solution)/shard_map/while/body/eval_jaxpr/reduce_sum | solution.py:63
  54.3 15.1 %select_reduce_fusion.2 = s32[1536]{0:T(1024)S(1)} fusion(s32[16384]{0:T(1024)S(1)} %get-tuple-element.266, s32[16384]{0:T(1024)S(1)} %get-tuple-element.265, s32[1536]{0:T(1024)S(1)} %iota_add_fusion.2), kind=kLoop, calls=%fused_computation.2.clone.1 | loop fusion | flops 75495936 | bytes 143360 | tf_op jit(solution)/shard_map/while/body/eval_jaxpr/reduce_sum | solution.py:63
  71.0 15.1 %select_reduce_fusion.2 = s32[1536]{0:T(1024)S(1)} fusion(s32[16384]{0:T(1024)S(1)} %get-tuple-element.266, s32[16384]{0:T(1024)S(1)} %get-tuple-element.265, s32[1536]{0:T(1024)S(1)} %iota_add_fusion.2), kind=kLoop, calls=%fused_computation.2.clone.1 | loop fusion | flops 75495936 | bytes 143360 | tf_op jit(solution)/shard_map/while/body/eval_jaxpr/reduce_sum | solution.py:63
  87.7 15.1 %select_reduce_fusion.2 = s32[1536]{0:T(1024)S(1)} fusion(s32[16384]{0:T(1024)S(1)} %get-tuple-element.266, s32[16384]{0:T(1024)S(1)} %get-tuple-element.265, s32[1536]{0:T(1024)S(1)} %iota_add_fusion.2), kind=kLoop, calls=%fused_computation.2.clone.1 | loop fusion | flops 75495936 | bytes 143360 | tf_op jit(solution)/shard_map/while/body/eval_jaxpr/reduce_sum | solution.py:63
  104.4 15.1 %select_reduce_fusion.2 = s32[1536]{0:T(1024)S(1)} fusion(s32[16384]{0:T(1024)S(1)} %get-tuple-element.266, s32[16384]{0:T(1024)S(1)} %get-tuple-element.265, s32[1536]{0:T(1024)S(1)} %iota_add_fusion.2), kind=kLoop, calls=%fused_computation.2.clone.1 | loop fusion | flops 75495936 | bytes 143360 | tf_op jit(solution)/shard_map/while/body/eval_jaxpr/reduce_sum | solution.py:63
  121.0 15.1 %select_reduce_fusion.2 = s32[1536]{0:T(1024)S(1)} fusion(s32[16384]{0:T(1024)S(1)} %get-tuple-element.266, s32[16384]{0:T(1024)S(1)} %get-tuple-element.265, s32[1536]{0:T(1024)S(1)} %iota_add_fusion.2), kind=kLoop, calls=%fused_computation.2.clone.1 | loop fusion | flops 75495936 | bytes 143360 | tf_op jit(solution)/shard_map/while/body/eval_jaxpr/reduce_sum | solution.py:63
  137.7 15.1 %select_reduce_fusion.2 = s32[1536]{0:T(1024)S(1)} fusion(s32[16384]{0:T(1024)S(1)} %get-tuple-element.266, s32[16384]{0:T(1024)S(1)} %get-tuple-element.265, s32[1536]{0:T(1024)S(1)} %iota_add_fusion.2), kind=kLoop, calls=%fused_computation.2.clone.1 | loop fusion | flops 75495936 | bytes 143360 | tf_op jit(solution)/shard_map/while/body/eval_jaxpr/reduce_sum | solution.py:63
  154.4 15.1 %select_reduce_fusion.2 = s32[1536]{0:T(1024)S(1)} fusion(s32[16384]{0:T(1024)S(1)} %get-tuple-element.266, s32[16384]{0:T(1024)S(1)} %get-tuple-element.265, s32[1536]{0:T(1024)S(1)} %iota_add_fusion.2), kind=kLoop, calls=%fused_computation.2.clone.1 | loop fusion | flops 75495936 | bytes 143360 | tf_op jit(solution)/shard_map/while/body/eval_jaxpr/reduce_sum | solution.py:63
  171.1 15.1 %select_reduce_fusion.2 = s32[1536]{0:T(1024)S(1)} fusion(s32[16384]{0:T(1024)S(1)} %get-tuple-element.266, s32[16384]{0:T(1024)S(1)} %get-tuple-element.265, s32[1536]{0:T(1024)S(1)} %iota_add_fusion.2), kind=kLoop, calls=%fused_computation.2.clone.1 | loop fusion | flops 75495936 | bytes 143360 | tf_op jit(solution)/shard_map/while/body/eval_jaxpr/reduce_sum | solution.py:63
  187.8 15.1 %select_reduce_fusion.2 = s32[1536]{0:T(1024)S(1)} fusion(s32[16384]{0:T(1024)S(1)} %get-tuple-element.266, s32[16384]{0:T(1024)S(1)} %get-tuple-element.265, s32[1536]{0:T(1024)S(1)} %iota_add_fusion.2), kind=kLoop, calls=%fused_computation.2.clone.1 | loop fusion | flops 75495936 | bytes 143360 | tf_op jit(solution)/shard_map/while/body/eval_jaxpr/reduce_sum | solution.py:63
  204.5 15.1 %select_reduce_fusion.2 = s32[1536]{0:T(1024)S(1)} fusion(s32[16384]{0:T(1024)S(1)} %get-tuple-element.266, s32[16384]{0:T(1024)S(1)} %get-tuple-element.265, s32[1536]{0:T(1024)S(1)} %iota_add_fusion.2), kind=kLoop, calls=%fused_computation.2.clone.1 | loop fusion | flops 75495936 | bytes 143360 | tf_op jit(solution)/shard_map/while/body/eval_jaxpr/reduce_sum | solution.py:63
  221.2 15.1 %select_reduce_fusion.2 = s32[1536]{0:T(1024)S(1)} fusion(s32[16384]{0:T(1024)S(1)} %get-tuple-element.266, s32[16384]{0:T(1024)S(1)} %get-tuple-element.265, s32[1536]{0:T(1024)S(1)} %iota_add_fusion.2), kind=kLoop, calls=%fused_computation.2.clone.1 | loop fusion | flops 75495936 | bytes 143360 | tf_op jit(solution)/shard_map/while/body/eval_jaxpr/reduce_sum | solution.py:63
  237.9 15.1 %select_reduce_fusion.2 = s32[1536]{0:T(1024)S(1)} fusion(s32[16384]{0:T(1024)S(1)} %get-tuple-element.266, s32[16384]{0:T(1024)S(1)} %get-tuple-element.265, s32[1536]{0:T(1024)S(1)} %iota_add_fusion.2), kind=kLoop, calls=%fused_computation.2.clone.1 | loop fusion | flops 75495936 | bytes 143360 | tf_op jit(solution)/shard_map/while/body/eval_jaxpr/reduce_sum | solution.py:63
  254.6 15.1 %select_reduce_fusion.2 = s32[1536]{0:T(1024)S(1)} fusion(s32[16384]{0:T(1024)S(1)} %get-tuple-element.266, s32[16384]{0:T(1024)S(1)} %get-tuple-element.265, s32[1536]{0:T(1024)S(1)} %iota_add_fusion.2), kind=kLoop, calls=%fused_computation.2.clone.1 | loop fusion | flops 75495936 | bytes 143360 | tf_op jit(solution)/shard_map/while/body/eval_jaxpr/reduce_sum | solution.py:63
  270.6 6.0 all-to-all-start
  276.7 24.5 %reshape.187 = bf16[16384,512]{1,0:T(8,128)(2,1)} reshape(bf16[32768,256]{1,0:T(8,128)(2,1)} %param.14) | data formatting | bytes 33554432 | tf_op jit(solution)/shard_map/reshape | solution.py:79
  301.3 19.1 %gather_fusion.1 = bf16[3072,512]{1,0:T(8,128)(2,1)S(1)} fusion(bf16[16384,512]{1,0:T(8,128)(2,1)} %reshape.187, s32[3072]{0:T(1024)S(1)} %broadcast_clamp_fusion.1), kind=kCustom, calls=%fused_computation.1 | custom fusion | bytes 6303744 | tf_op jit(solution)/shard_map/gather | solution.py:88
  320.6 27.6 %all_to_all.32 = bf16[16,1,96,512]{3,2,1,0:T(8,128)(2,1)S(1)} all-to-all(bf16[16,1,96,512]{3,2,1,0:T(8,128)(2,1)S(1)} %get-tuple-element.154), channel_id=1, replica_groups=mesh['beam'=16,'hid'=8] {'beam'}, dimensions={0} | all-to-all | bytes 3145728 | tf_op jit(solution)/shard_map/all_to_all | solution.py:32
  348.2 24.7 %all_to_all.33 = bf16[16,1,96,512]{3,2,1,0:T(8,128)(2,1)S(1)} all-to-all(bf16[16,1,96,512]{3,2,1,0:T(8,128)(2,1)S(1)} %get-tuple-element.155), channel_id=1, replica_groups=mesh['beam'=16,'hid'=8] {'beam'}, dimensions={0} | all-to-all | bytes 3145728 | tf_op jit(solution)/shard_map/all_to_all | solution.py:32
  373.2 8.6 stack.3
  381.8 7.5 all-to-all-start.3
  390.0 0.7 convolution_add_fusion.2
  390.8 338.2 %all-to-all-done.3 = bf16[8,16,192,512]{3,2,1,0:T(8,128)(2,1)} async-done(((bf16[8,16,192,512]{3,2,1,0:T(8,128)(2,1)}), bf16[8,16,192,512]{3,2,1,0:T(8,128)(2,1)}, u32[]{:S(2)}, u32[]{:S(2)}) %all-to-all-start.3) | async-done | bytes 25165856 | tf_op jit(solution)/shard_map/all_to_all | solution.py:91
  729.0 21.0 %copy.21 = bf16[8,16,192,512]{3,2,0,1:T(8,128)(2,1)} copy(bf16[8,16,192,512]{3,2,1,0:T(8,128)(2,1)} %all-to-all-done.3) | data formatting | bytes 50331648 | tf_op jit(solution)/shard_map/all_to_all | solution.py:91
  750.0 305.7 %while.21 = (s32[]{:T(128)}, f32[16,4,512]{2,1,0:T(4,128)S(1)}, s32[16,1024]{1,0:T(8,128)S(1)}, bf16[24576,512]{1,0:T(8,128)(2,1)}, bf16[256,128]{1,0:T(8,128)(2...) while((s32[]{:T(128)}, f32[16,4,512]{2,1,0:T(4,128)S(1)}, ...), condition=%wide.region_8.9_spmd, body=%wide.region_6.8_spmd.sunk | while | flops 271322112 | bytes 14893685 | solution.py:112
  750.0 15.4 %gather_fusion = bf16[1024,512]{1,0:T(8,128)(2,1)S(1)} fusion(bf16[24576,512]{1,0:T(8,128)(2,1)} %get-tuple-element.293, s32[1024]{0:T(1024)S(1)} %broadcast_clamp_fusion.3), kind=kCustom, calls=%fused_computation.clone.1 | custom fusion | bytes 2101248 | tf_op jit(solution)/shard_map/while/body/eval_jaxpr/gather | solution.py:100
  769.2 15.4 %gather_fusion = bf16[1024,512]{1,0:T(8,128)(2,1)S(1)} fusion(bf16[24576,512]{1,0:T(8,128)(2,1)} %get-tuple-element.293, s32[1024]{0:T(1024)S(1)} %broadcast_clamp_fusion.3), kind=kCustom, calls=%fused_computation.clone.1 | custom fusion | bytes 2101248 | tf_op jit(solution)/shard_map/while/body/eval_jaxpr/gather | solution.py:100
  788.2 15.4 %gather_fusion = bf16[1024,512]{1,0:T(8,128)(2,1)S(1)} fusion(bf16[24576,512]{1,0:T(8,128)(2,1)} %get-tuple-element.293, s32[1024]{0:T(1024)S(1)} %broadcast_clamp_fusion.3), kind=kCustom, calls=%fused_computation.clone.1 | custom fusion | bytes 2101248 | tf_op jit(solution)/shard_map/while/body/eval_jaxpr/gather | solution.py:100
  807.4 15.4 %gather_fusion = bf16[1024,512]{1,0:T(8,128)(2,1)S(1)} fusion(bf16[24576,512]{1,0:T(8,128)(2,1)} %get-tuple-element.293, s32[1024]{0:T(1024)S(1)} %broadcast_clamp_fusion.3), kind=kCustom, calls=%fused_computation.clone.1 | custom fusion | bytes 2101248 | tf_op jit(solution)/shard_map/while/body/eval_jaxpr/gather | solution.py:100
  826.5 15.4 %gather_fusion = bf16[1024,512]{1,0:T(8,128)(2,1)S(1)} fusion(bf16[24576,512]{1,0:T(8,128)(2,1)} %get-tuple-element.293, s32[1024]{0:T(1024)S(1)} %broadcast_clamp_fusion.3), kind=kCustom, calls=%fused_computation.clone.1 | custom fusion | bytes 2101248 | tf_op jit(solution)/shard_map/while/body/eval_jaxpr/gather | solution.py:100
  845.5 15.4 %gather_fusion = bf16[1024,512]{1,0:T(8,128)(2,1)S(1)} fusion(bf16[24576,512]{1,0:T(8,128)(2,1)} %get-tuple-element.293, s32[1024]{0:T(1024)S(1)} %broadcast_clamp_fusion.3), kind=kCustom, calls=%fused_computation.clone.1 | custom fusion | bytes 2101248 | tf_op jit(solution)/shard_map/while/body/eval_jaxpr/gather | solution.py:100
  864.7 15.4 %gather_fusion = bf16[1024,512]{1,0:T(8,128)(2,1)S(1)} fusion(bf16[24576,512]{1,0:T(8,128)(2,1)} %get-tuple-element.293, s32[1024]{0:T(1024)S(1)} %broadcast_clamp_fusion.3), kind=kCustom, calls=%fused_computation.clone.1 | custom fusion | bytes 2101248 | tf_op jit(solution)/shard_map/while/body/eval_jaxpr/gather | solution.py:100
  883.7 15.4 %gather_fusion = bf16[1024,512]{1,0:T(8,128)(2,1)S(1)} fusion(bf16[24576,512]{1,0:T(8,128)(2,1)} %get-tuple-element.293, s32[1024]{0:T(1024)S(1)} %broadcast_clamp_fusion.3), kind=kCustom, calls=%fused_computation.clone.1 | custom fusion | bytes 2101248 | tf_op jit(solution)/shard_map/while/body/eval_jaxpr/gather | solution.py:100
  902.9 15.4 %gather_fusion = bf16[1024,512]{1,0:T(8,128)(2,1)S(1)} fusion(bf16[24576,512]{1,0:T(8,128)(2,1)} %get-tuple-element.293, s32[1024]{0:T(1024)S(1)} %broadcast_clamp_fusion.3), kind=kCustom, calls=%fused_computation.clone.1 | custom fusion | bytes 2101248 | tf_op jit(solution)/shard_map/while/body/eval_jaxpr/gather | solution.py:100
  922.0 15.4 %gather_fusion = bf16[1024,512]{1,0:T(8,128)(2,1)S(1)} fusion(bf16[24576,512]{1,0:T(8,128)(2,1)} %get-tuple-element.293, s32[1024]{0:T(1024)S(1)} %broadcast_clamp_fusion.3), kind=kCustom, calls=%fused_computation.clone.1 | custom fusion | bytes 2101248 | tf_op jit(solution)/shard_map/while/body/eval_jaxpr/gather | solution.py:100
  941.1 15.4 %gather_fusion = bf16[1024,512]{1,0:T(8,128)(2,1)S(1)} fusion(bf16[24576,512]{1,0:T(8,128)(2,1)} %get-tuple-element.293, s32[1024]{0:T(1024)S(1)} %broadcast_clamp_fusion.3), kind=kCustom, calls=%fused_computation.clone.1 | custom fusion | bytes 2101248 | tf_op jit(solution)/shard_map/while/body/eval_jaxpr/gather | solution.py:100
  960.2 15.4 %gather_fusion = bf16[1024,512]{1,0:T(8,128)(2,1)S(1)} fusion(bf16[24576,512]{1,0:T(8,128)(2,1)} %get-tuple-element.293, s32[1024]{0:T(1024)S(1)} %broadcast_clamp_fusion.3), kind=kCustom, calls=%fused_computation.clone.1 | custom fusion | bytes 2101248 | tf_op jit(solution)/shard_map/while/body/eval_jaxpr/gather | solution.py:100
  979.3 15.4 %gather_fusion = bf16[1024,512]{1,0:T(8,128)(2,1)S(1)} fusion(bf16[24576,512]{1,0:T(8,128)(2,1)} %get-tuple-element.293, s32[1024]{0:T(1024)S(1)} %broadcast_clamp_fusion.3), kind=kCustom, calls=%fused_computation.clone.1 | custom fusion | bytes 2101248 | tf_op jit(solution)/shard_map/while/body/eval_jaxpr/gather | solution.py:100
  998.4 15.4 %gather_fusion = bf16[1024,512]{1,0:T(8,128)(2,1)S(1)} fusion(bf16[24576,512]{1,0:T(8,128)(2,1)} %get-tuple-element.293, s32[1024]{0:T(1024)S(1)} %broadcast_clamp_fusion.3), kind=kCustom, calls=%fused_computation.clone.1 | custom fusion | bytes 2101248 | tf_op jit(solution)/shard_map/while/body/eval_jaxpr/gather | solution.py:100
  1017.5 15.4 %gather_fusion = bf16[1024,512]{1,0:T(8,128)(2,1)S(1)} fusion(bf16[24576,512]{1,0:T(8,128)(2,1)} %get-tuple-element.293, s32[1024]{0:T(1024)S(1)} %broadcast_clamp_fusion.3), kind=kCustom, calls=%fused_computation.clone.1 | custom fusion | bytes 2101248 | tf_op jit(solution)/shard_map/while/body/eval_jaxpr/gather | solution.py:100
  1036.6 15.4 %gather_fusion = bf16[1024,512]{1,0:T(8,128)(2,1)S(1)} fusion(bf16[24576,512]{1,0:T(8,128)(2,1)} %get-tuple-element.293, s32[1024]{0:T(1024)S(1)} %broadcast_clamp_fusion.3), kind=kCustom, calls=%fused_computation.clone.1 | custom fusion | bytes 2101248 | tf_op jit(solution)/shard_map/while/body/eval_jaxpr/gather | solution.py:100
  1056.1 12.4 %all_to_all.34 = f32[8,1,4096]{2,1,0:T(1,128)S(1)} all-to-all(f32[8,1,4096]{2,1,0:T(1,128)S(1)} %reshape.214), channel_id=1, replica_groups=mesh['beam'=16,'hid'=8] {'hid'}, dimensions={0} | all-to-all | bytes 262144 | tf_op jit(solution)/shard_map/all_to_all | solution.py:38
  1069.0 1.0 reduce.4
  (317 shorter events, 76.3 us)
Async XLA Ops:
  0.0 390.0 %copy-start = (bf16[256,128]{1,0:T(8,128)(2,1)S(1)}, bf16[256,128]{1,0:T(8,128)(2,1)}, u32[]{:S(2)}) copy-start(bf16[256,128]{1,0:T(8,128)(2,1)} %param.15) | copy-start | bytes 196612
  270.6 30.6 %all-to-all-start = ((s32[16,1,192]{2,1,0:T(1,128)}), s32[16,1,192]{2,1,0:T(1,128)S(1)}, u32[]{:S(2)}, u32[]{:S(2)}) async-start(s32[16,1,192]{2,1,0:T(1,128)} %all_to_all.20), calls=%async_computation | async-start | bytes 32768 | tf_op jit(solution)/shard_map/all_to_all | solution.py:88
  381.8 7.5 copy-start.4
  381.8 7.5 copy-start.5
  381.8 8.2 copy-start.7
  381.8 347.2 %all-to-all-start.3 = ((bf16[8,16,192,512]{3,2,1,0:T(8,128)(2,1)}), bf16[8,16,192,512]{3,2,1,0:T(8,128)(2,1)}, u32[]{:S(2)}, u32[]{:S(2)}) async-start(bf16[8,16,192,512]{3,2,1,0:T(8,128)(2,1)} %stack.3), calls=%async_computation.3 | async-start | bytes 50331648 | tf_op jit(solution)/shard_map/all_to_all | solution.py:91
  390.8 359.2 %copy-start.2 = (bf16[256,128]{1,0:T(8,128)(2,1)S(1)}, bf16[256,128]{1,0:T(8,128)(2,1)}, u32[]{:S(2)}) copy-start(bf16[256,128]{1,0:T(8,128)(2,1)} %param.16) | copy-start | bytes 196612
  390.8 359.2 %copy-start.3 = (bf16[256,128]{1,0:T(8,128)(2,1)S(1)}, bf16[256,128]{1,0:T(8,128)(2,1)}, u32[]{:S(2)}) copy-start(bf16[256,128]{1,0:T(8,128)(2,1)} %param.17) | copy-start | bytes 196612
  390.8 359.2 %copy-start.6 = (f32[128]{0:T(128)S(1)}, f32[128]{0:T(128)}, u32[]{:S(2)}) copy-start(f32[128]{0:T(128)} %param.19) | copy-start | bytes 1540
  1055.7 15.0 %copy-start.1 = (bf16[256,128]{1,0:T(8,128)(2,1)S(1)}, bf16[256,128]{1,0:T(8,128)(2,1)}, u32[]{:S(2)}) copy-start(bf16[256,128]{1,0:T(8,128)(2,1)} %param.15) | copy-start | bytes 196612
